TPU v7x, 32 devices: a whole 2x2x4 slice. The times are simulated.
32 devices in a mesh: fsdp: 4 (over x, core), ctx: 8 (over z, y).
Axes of the slice: x: 2, y: 2, z: 4, core: 2. Of those that a mesh axis runs over, the one named last changes fastest.
Arguments:
- inputs: bfloat16 [4096, 1536], P(('fsdp', 'ctx')), may hold values from -6 to 6
- positions: int32 [4096], P(('fsdp', 'ctx')), may hold values from 0 to 1023, as said below
- cotangent: bfloat16 [4096, 1536], P(('fsdp', 'ctx')), may hold values from -6 to 6
- attention_gain: bfloat16 [1536], replicated, may hold values from 0.5 to 1.5
- query_weight: bfloat16 [1536, 1536], P('fsdp'), may hold values from -0.15625 to 0.15625
- key_weight: bfloat16 [768, 1536], P('fsdp'), may hold values from -0.15625 to 0.15625
- value_weight: bfloat16 [768, 1536], P('fsdp'), may hold values from -0.15625 to 0.15625
- output_weight: bfloat16 [1536, 1536], P('fsdp'), may hold values from -3 to 3
- feedforward_gain: bfloat16 [1536], replicated, may hold values from 0.5 to 1.5
- gate_weight: bfloat16 [4096, 1536], P('fsdp'), may hold values from -0.15625 to 0.15625
- up_weight: bfloat16 [4096, 1536], P('fsdp'), may hold values from -0.15625 to 0.15625
- down_weight: bfloat16 [4096, 1536], P('fsdp'), may hold values from -0.09375 to 0.09375
Outputs:
- layer_output: bfloat16 [4096, 1536], P(('fsdp', 'ctx'))
- input_grad: float32 [4096, 1536], P(('fsdp', 'ctx'))
- attention_gain_grad: float32 [1536], replicated
- query_weight_grad: float32 [1536, 1536], P('fsdp')
- key_weight_grad: float32 [768, 1536], P('fsdp')
- value_weight_grad: float32 [768, 1536], P('fsdp')
- output_weight_grad: float32 [1536, 1536], P('fsdp')
- feedforward_gain_grad: float32 [1536], replicated
- gate_weight_grad: float32 [4096, 1536], P('fsdp')
- up_weight_grad: float32 [4096, 1536], P('fsdp')
- down_weight_grad: float32 [4096, 1536], P('fsdp')
Inputs may be any that keep to these rules, and one draw needn't show every extreme that they name: Within each sequence every position appears once, and each device's 2 * 64 tokens of a sequence are two whole blocks of 64 consecutive rising positions, starting at b * 64 and at (15 - b) * 64 for some b, in either order.
All inputs are finite; a program needn't handle non-finite values.
Results may differ from a plain program's by a relative error of at most 0.022.
Values may be sent and summed in bfloat16 or wider, within the bound.
A program may use at most 384 MiB of HBM per device.

v0:
```python
import math
import jax
import jax.numpy as jnp
from jax import lax
from jax.sharding import PartitionSpec as P

HEADS = 16
KV_HEADS = 8
HEAD_DIM = 96
EPSILON = 1e-05
ROPE_BASE = 100000.0


def product(left, right):
    return jnp.dot(left, right, preferred_element_type=jnp.float32)


def product_back(left, right):
    return lax.dot_general(
        left, right, (((1,), (1,)), ((), ())), preferred_element_type=jnp.float32
    )


def product_rows(left, right):
    return lax.dot_general(
        left, right, (((0,), (0,)), ((), ())), preferred_element_type=jnp.float32
    )


def rms_scale(values):
    return lax.rsqrt(jnp.mean(values * values, axis=-1, keepdims=True) + EPSILON)


def norm_back(scale_rows, unit_rows, grad_unit):
    return scale_rows * (
        grad_unit - unit_rows * jnp.mean(grad_unit * unit_rows, axis=-1, keepdims=True)
    )


def rotary_tables(places):
    half_width = HEAD_DIM // 2
    frequencies = ROPE_BASE ** (-(jnp.arange(half_width, dtype=jnp.float32) * 2.0 / HEAD_DIM))
    angles = places.astype(jnp.float32)[:, None] * frequencies[None, :]
    return (jnp.cos(angles)[:, None, :], jnp.sin(angles)[:, None, :])


def rotate(values, cosine, sine):
    half_width = values.shape[-1] // 2
    lower_half = values[..., :half_width]
    upper_half = values[..., half_width:]
    return jnp.concatenate(
        [lower_half * cosine - upper_half * sine, upper_half * cosine + lower_half * sine], axis=-1
    )


def rotate_back(grads, cosine, sine):
    half_width = grads.shape[-1] // 2
    lower_half = grads[..., :half_width]
    upper_half = grads[..., half_width:]
    return jnp.concatenate(
        [lower_half * cosine + upper_half * sine, upper_half * cosine - lower_half * sine], axis=-1
    )


def block_total_of(total_keys):
    return max(1, total_keys // 512)


def masked_scores(query_grouped, query_places, key_rows, key_places, start, width):
    key_part = lax.dynamic_slice_in_dim(key_rows, start, width, 1)
    place_part = lax.dynamic_slice_in_dim(key_places, start, width, 1)
    scores = jnp.einsum(
        "sqhgd,skhd->shgqk", query_grouped, key_part, preferred_element_type=jnp.float32
    )
    scores = scores * (1.0 / math.sqrt(HEAD_DIM))
    allowed = place_part[:, None, None, None, :] <= query_places[:, None, None, :, None]
    return jnp.where(allowed, scores, -1000000000.0)


def attend_forward(query_grouped, query_places, key_rows, value_rows, key_places):
    seq_count, row_count, head_groups, group_size = query_grouped.shape[:4]
    total_keys = key_rows.shape[1]
    block_total = block_total_of(total_keys)
    width = total_keys // block_total
    stat_shape = (seq_count, head_groups, group_size, row_count)

    def peak_step(index, carry):
        running_top, running_sum = carry
        scores = masked_scores(
            query_grouped, query_places, key_rows, key_places, index * width, width
        )
        new_top = jnp.maximum(running_top, jnp.max(scores, axis=-1))
        running_sum = running_sum * jnp.exp(running_top - new_top) + jnp.sum(
            jnp.exp(scores - new_top[..., None]), axis=-1
        )
        return (new_top, running_sum)

    running_top, running_sum = lax.fori_loop(
        0,
        block_total,
        peak_step,
        (jnp.full(stat_shape, -1e30, jnp.float32), jnp.zeros(stat_shape, jnp.float32)),
    )
    log_total = running_top + jnp.log(running_sum)

    def value_step(index, gathered):
        scores = masked_scores(
            query_grouped, query_places, key_rows, key_places, index * width, width
        )
        soft_low = jnp.exp(scores - log_total[..., None]).astype(jnp.bfloat16)
        value_part = lax.dynamic_slice_in_dim(value_rows, index * width, width, 1)
        return gathered + jnp.einsum(
            "shgqk,skhd->sqhgd", soft_low, value_part, preferred_element_type=jnp.float32
        )

    attended = lax.fori_loop(
        0, block_total, value_step, jnp.zeros(query_grouped.shape, jnp.float32)
    )
    return (attended, log_total)


def attend_backward(
    query_grouped, query_places, key_rows, value_rows, key_places, log_total, grad_attended
):
    total_keys = key_rows.shape[1]
    block_total = block_total_of(total_keys)
    width = total_keys // block_total
    score_scale = 1.0 / math.sqrt(HEAD_DIM)

    def soft_and_grad(index):
        scores = masked_scores(
            query_grouped, query_places, key_rows, key_places, index * width, width
        )
        soft_values = jnp.exp(scores - log_total[..., None])
        value_part = lax.dynamic_slice_in_dim(value_rows, index * width, width, 1)
        grad_soft = jnp.einsum(
            "sqhgd,skhd->shgqk", grad_attended, value_part, preferred_element_type=jnp.float32
        )
        return (soft_values, grad_soft)

    def delta_step(index, row_delta):
        soft_values, grad_soft = soft_and_grad(index)
        return row_delta + jnp.sum(soft_values * grad_soft, axis=-1)

    row_delta = lax.fori_loop(0, block_total, delta_step, jnp.zeros(log_total.shape, jnp.float32))

    def grad_step(index, carry):
        grad_query, grad_keys, grad_values = carry
        soft_values, grad_soft = soft_and_grad(index)
        grad_scores = (soft_values * (grad_soft - row_delta[..., None])).astype(jnp.bfloat16)
        key_part = lax.dynamic_slice_in_dim(key_rows, index * width, width, 1)
        grad_query = (
            grad_query
            + jnp.einsum(
                "shgqk,skhd->sqhgd", grad_scores, key_part, preferred_element_type=jnp.float32
            )
            * score_scale
        )
        key_term = (
            jnp.einsum(
                "shgqk,sqhgd->skhd", grad_scores, query_grouped, preferred_element_type=jnp.float32
            )
            * score_scale
        )
        value_term = jnp.einsum(
            "shgqk,sqhgd->skhd",
            soft_values.astype(jnp.bfloat16),
            grad_attended,
            preferred_element_type=jnp.float32,
        )
        grad_keys = lax.dynamic_update_slice_in_dim(grad_keys, key_term, index * width, 1)
        grad_values = lax.dynamic_update_slice_in_dim(grad_values, value_term, index * width, 1)
        return (grad_query, grad_keys, grad_values)

    initial = (
        jnp.zeros(query_grouped.shape, jnp.float32),
        jnp.zeros(key_rows.shape, jnp.float32),
        jnp.zeros(value_rows.shape, jnp.float32),
    )
    return lax.fori_loop(0, block_total, grad_step, initial)


def per_device(
    inputs,
    positions,
    cotangent,
    attention_gain,
    query_weight,
    key_weight,
    value_weight,
    output_weight,
    feedforward_gain,
    gate_weight,
    up_weight,
    down_weight,
):
    row_count = inputs.shape[0]
    groups = HEADS // KV_HEADS
    gain_one = attention_gain.astype(jnp.float32)
    gain_two = feedforward_gain.astype(jnp.float32)
    seq_count = 1

    def attention_set():
        return (
            lax.all_gather(query_weight, "fsdp", axis=0, tiled=True),
            lax.all_gather(key_weight, "fsdp", axis=0, tiled=True),
            lax.all_gather(value_weight, "fsdp", axis=0, tiled=True),
            lax.all_gather(output_weight, "fsdp", axis=0, tiled=True),
        )

    def feedforward_set():
        return (
            lax.all_gather(gate_weight, "fsdp", axis=0, tiled=True),
            lax.all_gather(up_weight, "fsdp", axis=0, tiled=True),
            lax.all_gather(down_weight, "fsdp", axis=0, tiled=True),
        )

    query_places = positions.reshape(1, row_count)
    key_places = lax.all_gather(positions, "ctx", axis=0, tiled=True).reshape(1, -1)
    flat_in = inputs.astype(jnp.float32)
    scale_one = rms_scale(flat_in)
    unit_one = flat_in * scale_one
    normed_one = (unit_one * gain_one).astype(jnp.bfloat16)
    total_rows = normed_one.shape[0]
    cosine, sine = rotary_tables(query_places.reshape(-1))
    fwd_query, fwd_key, fwd_value, fwd_output = attention_set()
    query_heads = fwd_query.shape[0] // HEAD_DIM
    kv_heads = fwd_key.shape[0] // HEAD_DIM
    kv_width = kv_heads * HEAD_DIM
    query_low = rotate(
        product_back(normed_one, fwd_query).reshape(total_rows, query_heads, HEAD_DIM), cosine, sine
    ).astype(jnp.bfloat16)
    key_low = rotate(
        product_back(normed_one, fwd_key).reshape(total_rows, kv_heads, HEAD_DIM), cosine, sine
    ).astype(jnp.bfloat16)
    value_low = product_back(normed_one, fwd_value).astype(jnp.bfloat16)
    all_keys, all_values = (
        lax.all_gather(key_low.reshape(seq_count, row_count, kv_width), "ctx", axis=1, tiled=True),
        lax.all_gather(
            value_low.reshape(seq_count, row_count, kv_width), "ctx", axis=1, tiled=True
        ),
    )
    total_keys = all_keys.shape[1]
    key_grid = all_keys.reshape(seq_count, total_keys, kv_heads, HEAD_DIM)
    value_grid = all_values.reshape(seq_count, total_keys, kv_heads, HEAD_DIM)
    query_grouped = query_low.reshape(seq_count, row_count, kv_heads, groups, HEAD_DIM)
    attended, log_total = attend_forward(
        query_grouped, query_places, key_grid, value_grid, key_places
    )
    attended_low = attended.reshape(total_rows, query_heads * HEAD_DIM).astype(jnp.bfloat16)
    hidden_state = flat_in + product(attended_low, fwd_output)
    scale_two = rms_scale(hidden_state)
    unit_two = hidden_state * scale_two
    normed_two = (unit_two * gain_two).astype(jnp.bfloat16)
    fwd_gate, fwd_up, fwd_down = feedforward_set()
    gate_values = product_back(normed_two, fwd_gate)
    upward = product_back(normed_two, fwd_up)
    sigmoid_gate = jax.nn.sigmoid(gate_values)
    activated = gate_values * sigmoid_gate
    mixed_hidden = (activated * upward).astype(jnp.bfloat16)
    layer_output = (hidden_state + product(mixed_hidden, fwd_down)).astype(jnp.bfloat16)
    grad_out = cotangent.astype(jnp.float32)
    back_gate, back_up, back_down = feedforward_set()
    grad_down = product_rows(mixed_hidden, cotangent)
    grad_mixed = product_back(cotangent, back_down)
    grad_gate_low = (
        grad_mixed * upward * sigmoid_gate * (1.0 + gate_values * (1.0 - sigmoid_gate))
    ).astype(jnp.bfloat16)
    grad_up_low = (grad_mixed * activated).astype(jnp.bfloat16)
    grad_gate = product_rows(grad_gate_low, normed_two)
    grad_up = product_rows(grad_up_low, normed_two)
    feedforward_shards = (
        lax.psum_scatter(
            grad_gate.astype(jnp.bfloat16), "fsdp", scatter_dimension=0, tiled=True
        ).astype(jnp.float32),
        lax.psum_scatter(
            grad_up.astype(jnp.bfloat16), "fsdp", scatter_dimension=0, tiled=True
        ).astype(jnp.float32),
        lax.psum_scatter(
            grad_down.astype(jnp.bfloat16), "fsdp", scatter_dimension=0, tiled=True
        ).astype(jnp.float32),
    )
    grad_normed_two = product(grad_gate_low, back_gate) + product(grad_up_low, back_up)
    gain_two_grad = jnp.sum(grad_normed_two * unit_two, axis=0)
    grad_hidden = grad_out + norm_back(scale_two, unit_two, grad_normed_two * gain_two)
    branch_rows = grad_hidden.astype(jnp.bfloat16)
    back_query, back_key, back_value, back_output = attention_set()
    grad_output = product_rows(attended_low, branch_rows)
    grad_attended = product_back(branch_rows, back_output).astype(jnp.bfloat16)
    grad_attended = grad_attended.reshape(seq_count, row_count, kv_heads, groups, HEAD_DIM)
    grad_query_rot, grad_key_all, grad_value_all = attend_backward(
        query_grouped, query_places, key_grid, value_grid, key_places, log_total, grad_attended
    )
    key_grad_own, value_grad_own = (
        lax.psum_scatter(
            grad_key_all.reshape(seq_count, total_keys, kv_width).astype(jnp.bfloat16),
            "ctx",
            scatter_dimension=1,
            tiled=True,
        ).astype(jnp.float32),
        lax.psum_scatter(
            grad_value_all.reshape(seq_count, total_keys, kv_width).astype(jnp.bfloat16),
            "ctx",
            scatter_dimension=1,
            tiled=True,
        ).astype(jnp.float32),
    )
    grad_query_low = (
        rotate_back(grad_query_rot.reshape(total_rows, query_heads, HEAD_DIM), cosine, sine)
        .reshape(total_rows, query_heads * HEAD_DIM)
        .astype(jnp.bfloat16)
    )
    grad_key_low = (
        rotate_back(key_grad_own.reshape(total_rows, kv_heads, HEAD_DIM), cosine, sine)
        .reshape(total_rows, kv_width)
        .astype(jnp.bfloat16)
    )
    grad_value_low = value_grad_own.reshape(total_rows, kv_width).astype(jnp.bfloat16)
    grad_query = product_rows(grad_query_low, normed_one)
    grad_key = product_rows(grad_key_low, normed_one)
    grad_value = product_rows(grad_value_low, normed_one)
    attention_shards = (
        lax.psum_scatter(
            grad_query.astype(jnp.bfloat16), "fsdp", scatter_dimension=0, tiled=True
        ).astype(jnp.float32),
        lax.psum_scatter(
            grad_key.astype(jnp.bfloat16), "fsdp", scatter_dimension=0, tiled=True
        ).astype(jnp.float32),
        lax.psum_scatter(
            grad_value.astype(jnp.bfloat16), "fsdp", scatter_dimension=0, tiled=True
        ).astype(jnp.float32),
        lax.psum_scatter(
            grad_output.astype(jnp.bfloat16), "fsdp", scatter_dimension=0, tiled=True
        ).astype(jnp.float32),
    )
    grad_normed_one = (
        product(grad_query_low, back_query)
        + product(grad_key_low, back_key)
        + product(grad_value_low, back_value)
    )
    gain_one_grad = jnp.sum(grad_normed_one * unit_one, axis=0)
    input_grad = grad_hidden + norm_back(scale_one, unit_one, grad_normed_one * gain_one)
    summed = (
        lax.psum(attention_shards[0].astype(jnp.bfloat16), "ctx").astype(jnp.float32),
        lax.psum(attention_shards[1].astype(jnp.bfloat16), "ctx").astype(jnp.float32),
        lax.psum(attention_shards[2].astype(jnp.bfloat16), "ctx").astype(jnp.float32),
        lax.psum(attention_shards[3].astype(jnp.bfloat16), "ctx").astype(jnp.float32),
        lax.psum(feedforward_shards[0].astype(jnp.bfloat16), "ctx").astype(jnp.float32),
        lax.psum(feedforward_shards[1].astype(jnp.bfloat16), "ctx").astype(jnp.float32),
        lax.psum(feedforward_shards[2].astype(jnp.bfloat16), "ctx").astype(jnp.float32),
    )
    gain_sums = lax.psum((gain_one_grad, gain_two_grad), ("fsdp", "ctx"))
    return (
        layer_output,
        input_grad,
        gain_sums[0],
        summed[0],
        summed[1],
        summed[2],
        summed[3],
        gain_sums[1],
        summed[4],
        summed[5],
        summed[6],
    )


def solution(mesh):
    in_specs = (
        P(("fsdp", "ctx"), None),
        P(("fsdp", "ctx")),
        P(("fsdp", "ctx"), None),
        P(),
        P("fsdp", None),
        P("fsdp", None),
        P("fsdp", None),
        P("fsdp", None),
        P(),
        P("fsdp", None),
        P("fsdp", None),
        P("fsdp", None),
    )
    out_specs = (
        P(("fsdp", "ctx"), None),
        P(("fsdp", "ctx"), None),
        P(),
        P("fsdp", None),
        P("fsdp", None),
        P("fsdp", None),
        P("fsdp", None),
        P(),
        P("fsdp", None),
        P("fsdp", None),
        P("fsdp", None),
    )
    return jax.shard_map(
        per_device, mesh=mesh, in_specs=in_specs, out_specs=out_specs, check_vma=False
    )
```

profile of v0, /device:TPU:0, one launch (start us, length us, event | category | flops | bytes accessed | tf_op | source)
XLA Modules:
  0.0 1605.2 jit_solution(15687253532271398078)
XLA Ops:
  10.6 25.8 %all-gather.12.cloned.1.call-done = bf16[768,1536]{1,0:T(8,128)(2,1)} async-done(((bf16[192,1536]{1,0:T(8,128)(2,1)}), bf16[768,1536]{1,0:T(8,128)(2,1)}) %all-gather.12.cloned.1.call-update) | async-done | bytes 2359312 | tf_op jit(solution)/shard_map/all_gather | solution.py:207
  36.4 3.4 convolution_convert_fusion.8
  40.6 21.4 %all-gather.14.cloned.1.call-done = bf16[768,1536]{1,0:T(8,128)(2,1)} async-done(((bf16[192,1536]{1,0:T(8,128)(2,1)}), bf16[768,1536]{1,0:T(8,128)(2,1)}) %all-gather.14.cloned.1.call-update) | async-done | bytes 2359312 | tf_op jit(solution)/shard_map/all_gather | solution.py:206
  62.0 2.5 fusion.108
  68.2 20.5 %all-gather.1 = s32[8,1,128]{2,1,0:T(1,128)S(1)} all-gather(s32[1,1,128]{2,1,0:T(1,128)S(1)} %bitcast.402), channel_id=1, replica_groups=mesh['fsdp'=4,'ctx'=8] {'ctx'}, dimensions={0}, use_global_device_ids=true | all-gather | bytes 4608 | tf_op jit(solution)/shard_map/all_gather | solution.py:219
  88.8 20.2 %all-gather.28.cloned.1.call-done = bf16[1024,768]{1,0:T(8,128)(2,1)} async-done(((bf16[128,768]{1,0:T(8,128)(2,1)}), bf16[1024,768]{1,0:T(8,128)(2,1)}) %all-gather.28.cloned.1.call-update) | async-done | bytes 1572880 | tf_op jit(solution)/shard_map/all_gather | solution.py:239
  110.7 35.5 %all-gather.18.cloned.1.call-done = bf16[1536,1536]{1,0:T(8,128)(2,1)} async-done(((bf16[384,1536]{1,0:T(8,128)(2,1)}), bf16[1536,1536]{1,0:T(8,128)(2,1)}) %all-gather.18.cloned.1.call-update) | async-done | bytes 4718608 | tf_op jit(solution)/shard_map/all_gather | solution.py:205
  146.2 3.8 fusion.106
  150.2 43.0 %all-gather.16.cloned.1.call-done = bf16[1,1024,768]{1,2,0:T(8,128)(2,1)} async-done(((bf16[1,128,768]{1,2,0:T(8,128)(2,1)}), bf16[1,1024,768]{1,2,0:T(8,128)(2,1)}) %all-gather.16.cloned.1.call-update) | async-done | bytes 1572880 | tf_op jit(solution)/shard_map/all_gather | solution.py:238
  193.1 14.8 while.62
  193.3 4.0 fusion.172
  197.3 3.3 exponential_reduce_fusion.2
  200.9 4.0 fusion.172
  204.9 3.0 exponential_reduce_fusion.2
  208.0 8.3 while.63
  208.2 3.6 fusion.177
  211.9 3.8 fusion.177
  218.6 11.6 all-gather.20.cloned.1.call-done
  230.2 3.2 multiply_reduce_fusion.2
  233.6 80.3 %all-gather.22.cloned.1.call-done = bf16[4096,1536]{1,0:T(8,128)(2,1)} async-done(((bf16[1024,1536]{1,0:T(8,128)(2,1)}), bf16[4096,1536]{1,0:T(8,128)(2,1)}) %all-gather.22.cloned.1.call-update) | async-done | bytes 12582928 | tf_op jit(solution)/shard_map/all_gather | solution.py:213
  313.9 10.0 fusion.111
  323.8 73.7 %all-gather.24.cloned.1.call-done = bf16[4096,1536]{1,0:T(8,128)(2,1)} async-done(((bf16[1024,1536]{1,0:T(8,128)(2,1)}), bf16[4096,1536]{1,0:T(8,128)(2,1)}) %all-gather.24.cloned.1.call-update) | async-done | bytes 12582928 | tf_op jit(solution)/shard_map/all_gather | solution.py:214
  397.5 10.0 fusion.112
  407.5 73.7 %all-gather.26.cloned.1.call-done = bf16[4096,1536]{1,0:T(8,128)(2,1)} async-done(((bf16[1024,1536]{1,0:T(8,128)(2,1)}), bf16[4096,1536]{1,0:T(8,128)(2,1)}) %all-gather.26.cloned.1.call-update) | async-done | bytes 12582928 | tf_op jit(solution)/shard_map/all_gather | solution.py:215
  481.2 11.2 multiply_convert_fusion
  492.4 7.2 fusion.113
  499.6 6.7 multiply_reduce_fusion
  508.7 7.3 while.64
  512.4 2.0 fusion.182
  518.7 25.2 %while.65 = (s32[]{:T(128)}, f32[1,128,8,2,96]{1,4,3,2,0:T(8,128)}, bf16[1,1024,8,96]{1,3,2,0:T(8,128)(2,1)}, bf16[1,1024,8,96]{1,3,2,0:T(8,128)(2,1)}, bf16[1,1...) while((s32[]{:T(128)}, f32[1,128,8,2,96]{1,4,3,2,0:T(8,128)}, ...), condition=%wide.region_13.14_spmd.clone, body=%wide.region_12.13_spmd.clone.sunk | while | flops 1018167296 | bytes 70744944 | solution.py:180
  518.7 2.1 fusion.194
  520.9 2.8 fusion.195
  525.4 2.7 fusion.196
  528.1 3.0 bitcast_dynamic-update-slice_fusion.5
  531.1 2.1 fusion.194
  533.4 2.8 fusion.195
  537.9 2.9 fusion.196
  540.8 3.0 bitcast_dynamic-update-slice_fusion.5
  543.9 8.3 copy.69
  552.2 3.4 copy.78
  555.7 5.5 copy.71
  561.2 3.3 copy.77
  564.6 56.8 %reduce-scatter.28.cloned.1.call-done = bf16[128,768]{1,0:T(8,128)(2,1)} async-done(((bf16[1024,768]{1,0:T(8,128)(2,1)}), bf16[128,768]{1,0:T(8,128)(2,1)}) %reduce-scatter.28.cloned.1.call-update) | async-done | bytes 196624
  623.1 2.3 convolution_convert_fusion.6
  625.5 64.5 %reduce-scatter.30.cloned.1.call-done = bf16[128,768]{1,0:T(8,128)(2,1)} async-done(((bf16[1024,768]{1,0:T(8,128)(2,1)}), bf16[128,768]{1,0:T(8,128)(2,1)}) %reduce-scatter.30.cloned.1.call-update) | async-done | bytes 196624
  691.6 2.3 convolution_convert_fusion.5
  694.1 3.7 convolution_convert_fusion.4
  699.1 3.6 convolution_convert_fusion.3
  703.9 6.6 convolution_convert_fusion.2
  711.7 6.5 convolution_convert_fusion.1
  719.4 6.4 convolution_convert_fusion
  725.9 34.6 %reduce-scatter.18.cloned.1.call-done = bf16[192,1536]{1,0:T(8,128)(2,1)} async-done(((bf16[768,1536]{1,0:T(8,128)(2,1)}), bf16[192,1536]{1,0:T(8,128)(2,1)}) %reduce-scatter.18.cloned.1.call-update) | async-done | bytes 589840 | tf_op jit(solution)/shard_map/reduce_scatter | solution.py:329
  760.5 51.0 %reduce-scatter.14.cloned.1.call-done = bf16[384,1536]{1,0:T(8,128)(2,1)} async-done(((bf16[1536,1536]{1,0:T(8,128)(2,1)}), bf16[384,1536]{1,0:T(8,128)(2,1)}) %reduce-scatter.14.cloned.1.call-update) | async-done | bytes 1179664 | tf_op jit(solution)/shard_map/reduce_scatter | solution.py:323
  811.5 51.0 %reduce-scatter.20.cloned.1.call-done = bf16[384,1536]{1,0:T(8,128)(2,1)} async-done(((bf16[1536,1536]{1,0:T(8,128)(2,1)}), bf16[384,1536]{1,0:T(8,128)(2,1)}) %reduce-scatter.20.cloned.1.call-update) | async-done | bytes 1179664 | tf_op jit(solution)/shard_map/reduce_scatter | solution.py:332
  862.4 102.1 %reduce-scatter.22.cloned.1.call-done = bf16[1024,1536]{1,0:T(8,128)(2,1)} async-done(((bf16[4096,1536]{1,0:T(8,128)(2,1)}), bf16[1024,1536]{1,0:T(8,128)(2,1)}) %reduce-scatter.22.cloned.1.call-update) | async-done | bytes 3145744 | tf_op jit(solution)/shard_map/reduce_scatter | solution.py:273
  964.5 102.1 %reduce-scatter.24.cloned.1.call-done = bf16[1024,1536]{1,0:T(8,128)(2,1)} async-done(((bf16[4096,1536]{1,0:T(8,128)(2,1)}), bf16[1024,1536]{1,0:T(8,128)(2,1)}) %reduce-scatter.24.cloned.1.call-update) | async-done | bytes 3145744 | tf_op jit(solution)/shard_map/reduce_scatter | solution.py:276
  1066.6 102.1 %reduce-scatter.26.cloned.1.call-done = bf16[1024,1536]{1,0:T(8,128)(2,1)} async-done(((bf16[4096,1536]{1,0:T(8,128)(2,1)}), bf16[1024,1536]{1,0:T(8,128)(2,1)}) %reduce-scatter.26.cloned.1.call-update) | async-done | bytes 3145744 | tf_op jit(solution)/shard_map/reduce_scatter | solution.py:279
  1168.8 3.2 fusion.114
  1172.0 7.3 fusion.86
  1182.4 44.1 %all-reduce = (f32[1536]{0:T(1024)}, f32[1536]{0:T(1024)}) all-reduce(f32[1536]{0:T(1024)S(1)} %get-tuple-element.788, f32[1536]{0:T(1024)S(1)} %get-tuple-element.786), channel_id=1, replica_groups=mesh['fsdp'=4,'ctx'=8] {'fsdp','ctx'}, use_global_device_ids=true, to_apply=%region_18.19 | all-reduce | flops 3072 | bytes 24576 | tf_op jit(solution)/shard_map/psum | solution.py:352
  1227.7 352.3 %all-reduce.4.cloned.1.call-done = (bf16[384,1536]{1,0:T(8,128)(2,1)}, bf16[192,1536]{1,0:T(8,128)(2,1)}, bf16[192,1536]{1,0:T(8,128)(2,1)}, bf16[384,1536]{1,0:...) async-done(((bf16[384,1536]{1,0:T(8,128)(2,1)}, bf16[192,1536]{1,0:T(8,128)(2,1)}, bf16[192,1536]{1,0:T(8,128)(2,1)}, ...) | async-done | bytes 12976144 | tf_op jit(solution)/shard_map/psum | solution.py:344
  1580.0 5.6 convert_element_type.219
  1585.6 3.6 convert_element_type.221
  1589.2 3.6 convert_element_type.223
  (199 shorter events, 45.2 us)
Async XLA Ops:
  7.2 54.8 %copy-start.2 = (bf16[128,1536]{1,0:T(8,128)(2,1)S(1)}, bf16[128,1536]{1,0:T(8,128)(2,1)}, u32[]{:S(2)}) copy-start(bf16[128,1536]{1,0:T(8,128)(2,1)} %param.20) | copy-start | bytes 1179652
  7.2 33.2 %copy-start.33 = (s32[128]{0:T(128)S(1)}, s32[128]{0:T(128)}, u32[]{:S(2)}) copy-start(s32[128]{0:T(128)} %param.21) | copy-start | bytes 1540
  7.2 29.2 %all-gather.12.cloned.1.call-start = ((), (), s32[]{:S(2)}) async-start(), calls=%async_computation.9 | async-start | bytes 2949120 | tf_op jit(solution)/shard_map/all_gather | solution.py:207
  7.9 54.1 %all-gather.14.cloned.1.call-start = ((), (), s32[]{:S(2)}) async-start(), calls=%async_computation.10 | async-start | bytes 2949120 | tf_op jit(solution)/shard_map/all_gather | solution.py:206
  8.7 100.3 %all-gather.28.cloned.1.call-start = ((), (), s32[]{:S(2)}) async-start(), calls=%async_computation.24 | async-start | bytes 1769472 | tf_op jit(solution)/shard_map/all_gather | solution.py:239
  39.8 106.5 %all-gather.18.cloned.1.call-start = ((), (), s32[]{:S(2)}) async-start(), calls=%async_computation.12 | async-start | bytes 5898240 | tf_op jit(solution)/shard_map/all_gather | solution.py:205
  40.4 152.8 %all-gather.16.cloned.1.call-start = ((), (), s32[]{:S(2)}) async-start(), calls=%async_computation.11 | async-start | bytes 1769472 | tf_op jit(solution)/shard_map/all_gather | solution.py:238
  65.3 164.9 %all-gather.20.cloned.1.call-start = ((), (), s32[]{:S(2)}) async-start(), calls=%async_computation.13 | async-start | bytes 5898240 | tf_op jit(solution)/shard_map/all_gather | solution.py:208
  65.9 2.3 copy-start.34
  65.9 248.0 %all-gather.22.cloned.1.call-start = ((), (), s32[]{:S(2)}) async-start(), calls=%async_computation.14 | async-start | bytes 15728640 | tf_op jit(solution)/shard_map/all_gather | solution.py:213
  66.6 330.9 %all-gather.24.cloned.1.call-start = ((), (), s32[]{:S(2)}) async-start(), calls=%async_computation.15 | async-start | bytes 15728640 | tf_op jit(solution)/shard_map/all_gather | solution.py:214
  67.4 413.8 %all-gather.26.cloned.1.call-start = ((), (), s32[]{:S(2)}) async-start(), calls=%async_computation.16 | async-start | bytes 15728640 | tf_op jit(solution)/shard_map/all_gather | solution.py:215
  68.1 553.3 %reduce-scatter.28.cloned.1.call-start = ((), (), s32[]{:S(2)}) async-start(), calls=%async_computation.25 | async-start | bytes 1769472
  216.2 1.1 copy-start.22
  218.6 105.3 %copy-start.16 = (bf16[1,128,8,2,96]{1,4,3,2,0:T(8,128)(2,1)}, bf16[1,128,8,2,96]{1,4,3,2,0:T(8,128)(2,1)S(1)}, u32[]{:S(2)}) copy-start(bf16[1,128,8,2,96]{1,4,3,2,0:T(8,128)(2,1)S(1)} %convert_element_type.192) | copy-start | bytes 1179652
  233.4 272.9 %copy-start.4 = (f32[128,1536]{1,0:T(8,128)}, f32[128,1536]{1,0:T(8,128)S(1)}, u32[]{:S(2)}) copy-start(f32[128,1536]{1,0:T(8,128)S(1)} %get-tuple-element.887) | copy-start | bytes 2359300
  492.4 7.2 copy-start.12
  492.4 7.2 copy-start.10
  492.4 14.2 slice-start
  499.6 6.7 copy-start.25
  499.6 7.0 slice-start.1
  506.6 2.1 copy-start.6
  508.7 2.2 copy-start.23
  512.4 2.2 copy-start.23
  518.7 2.3 copy-start.31
  518.7 2.3 copy-start.24
  520.8 3.0 copy-start
  525.4 2.7 copy-start.1
  528.1 3.0 copy-start.32
  531.1 2.3 copy-start.31
  531.1 2.3 copy-start.24
  533.2 3.0 copy-start
  537.9 2.9 copy-start.1
  540.8 3.0 copy-start.32
  552.2 3.5 copy-start.15
  555.6 134.4 %reduce-scatter.30.cloned.1.call-start = ((), (), s32[]{:S(2)}) async-start(), calls=%async_computation.26 | async-start | bytes 1769472
  564.6 161.4 %reduce-scatter.16.cloned.1.call-start = ((), (), s32[]{:S(2)}) async-start(), calls=%async_computation.18 | async-start | bytes 2949120 | tf_op jit(solution)/shard_map/reduce_scatter | solution.py:326
  625.4 68.5 %copy-start.3 = (f32[1,128,8,2,96]{1,4,3,2,0:T(8,128)S(1)}, f32[1,128,8,2,96]{1,4,3,2,0:T(8,128)}, u32[]{:S(2)}) copy-start(f32[1,128,8,2,96]{1,4,3,2,0:T(8,128)} %get-tuple-element.634) | copy-start | bytes 2359300
  625.4 135.1 %reduce-scatter.18.cloned.1.call-start = ((), (), s32[]{:S(2)}) async-start(), calls=%async_computation.19 | async-start | bytes 2949120 | tf_op jit(solution)/shard_map/reduce_scatter | solution.py:329
  691.5 2.5 copy-start.20
  693.9 117.6 %reduce-scatter.14.cloned.1.call-start = ((), (), s32[]{:S(2)}) async-start(), calls=%async_computation.17 | async-start | bytes 5898240 | tf_op jit(solution)/shard_map/reduce_scatter | solution.py:323
  697.7 1.2 copy-start.7
  697.7 1.3 copy-start.17
  697.8 164.7 %reduce-scatter.20.cloned.1.call-start = ((), (), s32[]{:S(2)}) async-start(), calls=%async_computation.20 | async-start | bytes 5898240 | tf_op jit(solution)/shard_map/reduce_scatter | solution.py:332
  702.6 1.2 copy-start.13
  702.7 261.9 %reduce-scatter.22.cloned.1.call-start = ((), (), s32[]{:S(2)}) async-start(), calls=%async_computation.21 | async-start | bytes 15728640 | tf_op jit(solution)/shard_map/reduce_scatter | solution.py:273
  710.4 1.2 copy-start.11
  710.5 356.2 %reduce-scatter.24.cloned.1.call-start = ((), (), s32[]{:S(2)}) async-start(), calls=%async_computation.22 | async-start | bytes 15728640 | tf_op jit(solution)/shard_map/reduce_scatter | solution.py:276
  718.1 1.2 copy-start.14
  718.1 1.3 copy-start.26
  718.1 450.6 %reduce-scatter.26.cloned.1.call-start = ((), (), s32[]{:S(2)}) async-start(), calls=%async_computation.23 | async-start | bytes 15728640 | tf_op jit(solution)/shard_map/reduce_scatter | solution.py:279
  725.9 854.1 %all-reduce.4.cloned.1.call-start = ((), (), s32[]{:S(2)}) async-start(), calls=%async_computation.27 | async-start | bytes 25952256 | tf_op jit(solution)/shard_map/psum | solution.py:344
  1168.8 3.2 copy-start.5
  1172.0 7.3 copy-start.9
  1179.3 2.4 copy-start.8
  1179.3 2.4 copy-start.21
  1580.0 5.6 copy-start.19
  1585.6 3.6 copy-start.18
  1589.2 3.6 copy-start.28
  1589.2 5.3 copy-start.27
  1592.8 3.4 copy-start.30
  1592.8 4.5 copy-start.29
Sparse Core Ops, SparseCore 0:
  9.6 26.7 all-gather.11
  37.9 24.0 all-gather.13
  64.8 44.1 all-gather.27
  110.4 35.7 all-gather.17
  148.7 44.4 all-gather.15
  194.6 35.5 all-gather.19
  231.8 82.0 all-gather.21
  315.4 82.0 all-gather.23
  399.1 82.0 all-gather.25
  555.7 65.6 reduce-scatter.27
  625.4 64.5 reduce-scatter.29
  693.0 31.5 reduce-scatter.15
  727.7 32.8 reduce-scatter.17
  763.5 47.9 reduce-scatter.13
  814.4 47.9 reduce-scatter.19
  864.9 99.6 reduce-scatter.21
  967.0 99.6 reduce-scatter.23
  1069.1 99.6 reduce-scatter.25
  1174.4 405.4 all-reduce.3
where the time goes:
time: 1610 us
  waiting for transfers between devices  1310 us (81%)
  matrix products  149 us (9%)
  blocking collectives  64.7 us (4%)
  local copies, waits for them, and re-layouts  36.1 us (2%)
  other arithmetic  32 us (2%)
    psum x1, waiting for transfers between devices, per_device(): lax.psum(attention_shards[0].astype(jnp.bfloat16), 'ctx')  352 us
    unnamed x21, waiting for transfers between devices  126 us
    reduce_scatter x1, waiting for transfers between devices, per_device(): lax.psum_scatter(grad_gate.astype(jnp.bfloat16), 'fsdp', scatter_dimensio...  102 us
    reduce_scatter x1, waiting for transfers between devices, per_device(): lax.psum_scatter(grad_down.astype(jnp.bfloat16), 'fsdp', scatter_dimensio...  102 us
    reduce_scatter x1, waiting for transfers between devices, per_device(): lax.psum_scatter(grad_up.astype(jnp.bfloat16), 'fsdp', scatter_dimension=...  102 us
    all_gather x1, waiting for transfers between devices, feedforward_set(): lax.all_gather(gate_weight, 'fsdp', axis=0, tiled=True)  80.3 us
    all_gather x1, waiting for transfers between devices, feedforward_set(): lax.all_gather(down_weight, 'fsdp', axis=0, tiled=True)  73.7 us
    all_gather x1, waiting for transfers between devices, feedforward_set(): lax.all_gather(up_weight, 'fsdp', axis=0, tiled=True)  73.7 us
  transfers between devices with their start and end apart: 19, of which 18 were waited for; matrix products, arithmetic and copies ran while one was open for 7% of the time, Pallas kernels for 0%

commit v1 on v0

--- a/solution.py
+++ b/solution.py
@@ -3,6 +3,7 @@
 import jax.numpy as jnp
 from jax import lax
 from jax.sharding import PartitionSpec as P
+from jax.lax import all_gather
 
 HEADS = 16
 KV_HEADS = 8
@@ -341,7 +342,9 @@
     gain_one_grad = jnp.sum(grad_normed_one * unit_one, axis=0)
     input_grad = grad_hidden + norm_back(scale_one, unit_one, grad_normed_one * gain_one)
     summed = (
-        lax.psum(attention_shards[0].astype(jnp.bfloat16), "ctx").astype(jnp.float32),
+        jnp.sum(all_gather(attention_shards[0].astype(jnp.bfloat16), "ctx"), axis=0).astype(
+            jnp.float32
+        ),
         lax.psum(attention_shards[1].astype(jnp.bfloat16), "ctx").astype(jnp.float32),
         lax.psum(attention_shards[2].astype(jnp.bfloat16), "ctx").astype(jnp.float32),
         lax.psum(attention_shards[3].astype(jnp.bfloat16), "ctx").astype(jnp.float32),

time: 1610 us -> 1710 us (1.062)
  waiting for transfers between devices: 1310 us -> 1390 us
    all_gather x0 -> x1, waiting for transfers between devices: none -> 81.9 us  [per_device(): all_gather(attention_shards[0].astype(jnp.bfloat16), 'ctx')]
    reduce_scatter x1, waiting for transfers between devices: 0.02 us -> 35.9 us  [per_device(): lax.psum_scatter(grad_key.astype(jnp.bfloat16), 'fsdp', scatter_dimension...]
    reduce_scatter x1, waiting for transfers between devices: 51 us -> 18.5 us  [per_device(): lax.psum_scatter(grad_query.astype(jnp.bfloat16), 'fsdp', scatter_dimensi...]
    unnamed x21 -> x22, waiting for transfers between devices: 126 us -> 122 us
  transfers between devices with their start and end apart: 19 -> 20, of which waited for: 18 -> 20; matrix products, arithmetic and copies ran while one was open for 7% -> 7% of each run, Pallas kernels for 0% -> 0%
where the time goes in v1:
time: 1710 us; the launch traced here: 1700 us
  waiting for transfers between devices  1390 us (81%)
  matrix products  150 us (9%)
  blocking collectives  64.9 us (4%)
  other arithmetic  37.7 us (2%)
  local copies, waits for them, and re-layouts  34.6 us (2%)
    psum x1, waiting for transfers between devices, per_device(): lax.psum(attention_shards[1].astype(jnp.bfloat16), 'ctx')  358 us
    unnamed x22, waiting for transfers between devices  122 us
    reduce_scatter x1, waiting for transfers between devices, per_device(): lax.psum_scatter(grad_down.astype(jnp.bfloat16), 'fsdp', scatter_dimensio...  102 us
    reduce_scatter x1, waiting for transfers between devices, per_device(): lax.psum_scatter(grad_gate.astype(jnp.bfloat16), 'fsdp', scatter_dimensio...  102 us
    reduce_scatter x1, waiting for transfers between devices, per_device(): lax.psum_scatter(grad_up.astype(jnp.bfloat16), 'fsdp', scatter_dimension=...  102 us
    all_gather x1, waiting for transfers between devices, per_device(): all_gather(attention_shards[0].astype(jnp.bfloat16), 'ctx')  81.9 us
    all_gather x1, waiting for transfers between devices, feedforward_set(): lax.all_gather(gate_weight, 'fsdp', axis=0, tiled=True)  80.3 us
    all_gather x1, waiting for transfers between devices, feedforward_set(): lax.all_gather(down_weight, 'fsdp', axis=0, tiled=True)  73.7 us
  transfers between devices with their start and end apart: 20, of which 20 were waited for; matrix products, arithmetic and copies ran while one was open for 7% of the time, Pallas kernels for 0%

profile of v1, /device:TPU:0, one launch (start us, length us, event | category | flops | bytes accessed | tf_op | source)
XLA Modules:
  0.0 1698.9 jit_solution(11883376395268189844)
XLA Ops:
  10.6 25.8 %all-gather.14.cloned.1.call-done = bf16[768,1536]{1,0:T(8,128)(2,1)} async-done(((bf16[192,1536]{1,0:T(8,128)(2,1)}), bf16[768,1536]{1,0:T(8,128)(2,1)}) %all-gather.14.cloned.1.call-update) | async-done | bytes 2359312 | tf_op jit(solution)/shard_map/all_gather | solution.py:208
  36.4 3.4 convolution_convert_fusion.8
  40.6 21.4 %all-gather.16.cloned.1.call-done = bf16[768,1536]{1,0:T(8,128)(2,1)} async-done(((bf16[192,1536]{1,0:T(8,128)(2,1)}), bf16[768,1536]{1,0:T(8,128)(2,1)}) %all-gather.16.cloned.1.call-update) | async-done | bytes 2359312 | tf_op jit(solution)/shard_map/all_gather | solution.py:207
  62.0 2.5 fusion.108
  68.2 20.5 %all-gather.2 = s32[8,1,128]{2,1,0:T(1,128)S(1)} all-gather(s32[1,1,128]{2,1,0:T(1,128)S(1)} %bitcast.404), channel_id=1, replica_groups=mesh['fsdp'=4,'ctx'=8] {'ctx'}, dimensions={0}, use_global_device_ids=true | all-gather | bytes 4608 | tf_op jit(solution)/shard_map/all_gather | solution.py:220
  88.8 20.2 %all-gather.30.cloned.1.call-done = bf16[1024,768]{1,0:T(8,128)(2,1)} async-done(((bf16[128,768]{1,0:T(8,128)(2,1)}), bf16[1024,768]{1,0:T(8,128)(2,1)}) %all-gather.30.cloned.1.call-update) | async-done | bytes 1572880 | tf_op jit(solution)/shard_map/all_gather | solution.py:240
  110.7 35.5 %all-gather.20.cloned.1.call-done = bf16[1536,1536]{1,0:T(8,128)(2,1)} async-done(((bf16[384,1536]{1,0:T(8,128)(2,1)}), bf16[1536,1536]{1,0:T(8,128)(2,1)}) %all-gather.20.cloned.1.call-update) | async-done | bytes 4718608 | tf_op jit(solution)/shard_map/all_gather | solution.py:206
  146.2 3.8 fusion.106
  150.2 43.0 %all-gather.18.cloned.1.call-done = bf16[1,1024,768]{1,2,0:T(8,128)(2,1)} async-done(((bf16[1,128,768]{1,2,0:T(8,128)(2,1)}), bf16[1,1024,768]{1,2,0:T(8,128)(2,1)}) %all-gather.18.cloned.1.call-update) | async-done | bytes 1572880 | tf_op jit(solution)/shard_map/all_gather | solution.py:239
  193.1 14.8 while.62
  193.3 4.0 fusion.172
  197.3 3.3 exponential_reduce_fusion.2
  200.9 4.0 fusion.172
  204.9 3.0 exponential_reduce_fusion.2
  208.0 8.3 while.63
  208.2 3.6 fusion.177
  211.9 3.8 fusion.177
  218.6 11.6 all-gather.22.cloned.1.call-done
  230.2 3.2 multiply_reduce_fusion.2
  233.6 80.3 %all-gather.24.cloned.1.call-done = bf16[4096,1536]{1,0:T(8,128)(2,1)} async-done(((bf16[1024,1536]{1,0:T(8,128)(2,1)}), bf16[4096,1536]{1,0:T(8,128)(2,1)}) %all-gather.24.cloned.1.call-update) | async-done | bytes 12582928 | tf_op jit(solution)/shard_map/all_gather | solution.py:214
  313.9 10.0 fusion.111
  323.8 73.7 %all-gather.26.cloned.1.call-done = bf16[4096,1536]{1,0:T(8,128)(2,1)} async-done(((bf16[1024,1536]{1,0:T(8,128)(2,1)}), bf16[4096,1536]{1,0:T(8,128)(2,1)}) %all-gather.26.cloned.1.call-update) | async-done | bytes 12582928 | tf_op jit(solution)/shard_map/all_gather | solution.py:215
  397.5 10.0 fusion.112
  407.5 73.7 %all-gather.28.cloned.1.call-done = bf16[4096,1536]{1,0:T(8,128)(2,1)} async-done(((bf16[1024,1536]{1,0:T(8,128)(2,1)}), bf16[4096,1536]{1,0:T(8,128)(2,1)}) %all-gather.28.cloned.1.call-update) | async-done | bytes 12582928 | tf_op jit(solution)/shard_map/all_gather | solution.py:216
  481.2 11.2 multiply_convert_fusion
  492.4 7.2 fusion.113
  499.6 6.7 multiply_reduce_fusion
  508.7 7.3 while.64
  518.7 25.2 %while.65 = (s32[]{:T(128)}, f32[1,128,8,2,96]{1,4,3,2,0:T(8,128)}, bf16[1,1024,8,96]{1,3,2,0:T(8,128)(2,1)}, bf16[1,1024,8,96]{1,3,2,0:T(8,128)(2,1)}, bf16[1,1...) while((s32[]{:T(128)}, f32[1,128,8,2,96]{1,4,3,2,0:T(8,128)}, ...), condition=%wide.region_13.14_spmd.clone, body=%wide.region_12.13_spmd.clone.sunk | while | flops 1018167296 | bytes 70744944 | solution.py:181
  520.9 2.8 fusion.195
  525.4 2.7 fusion.196
  528.1 3.0 bitcast_dynamic-update-slice_fusion.5
  533.4 2.8 fusion.195
  537.9 2.9 fusion.196
  540.9 3.0 bitcast_dynamic-update-slice_fusion.5
  543.9 8.3 copy.69
  552.2 3.4 copy.78
  555.7 5.5 copy.71
  561.2 3.5 copy.77
  564.9 3.7 convolution_convert_fusion.4
  568.7 52.8 %reduce-scatter.28.cloned.1.call-done = bf16[128,768]{1,0:T(8,128)(2,1)} async-done(((bf16[1024,768]{1,0:T(8,128)(2,1)}), bf16[128,768]{1,0:T(8,128)(2,1)}) %reduce-scatter.28.cloned.1.call-update) | async-done | bytes 196624
  623.2 2.3 convolution_convert_fusion.6
  625.5 64.5 %reduce-scatter.30.cloned.1.call-done = bf16[128,768]{1,0:T(8,128)(2,1)} async-done(((bf16[1024,768]{1,0:T(8,128)(2,1)}), bf16[128,768]{1,0:T(8,128)(2,1)}) %reduce-scatter.30.cloned.1.call-update) | async-done | bytes 196624
  691.6 2.3 convolution_convert_fusion.5
  694.2 3.7 convolution_convert_fusion.3
  699.2 6.5 convolution_convert_fusion.2
  706.9 6.6 convolution_convert_fusion.1
  714.8 6.4 convolution_convert_fusion
  721.3 18.5 %reduce-scatter.14.cloned.1.call-done = bf16[384,1536]{1,0:T(8,128)(2,1)} async-done(((bf16[1536,1536]{1,0:T(8,128)(2,1)}), bf16[384,1536]{1,0:T(8,128)(2,1)}) %reduce-scatter.14.cloned.1.call-update) | async-done | bytes 1179664 | tf_op jit(solution)/shard_map/reduce_scatter | solution.py:324
  739.9 35.9 %reduce-scatter.16.cloned.1.call-done = bf16[192,1536]{1,0:T(8,128)(2,1)} async-done(((bf16[768,1536]{1,0:T(8,128)(2,1)}), bf16[192,1536]{1,0:T(8,128)(2,1)}) %reduce-scatter.16.cloned.1.call-update) | async-done | bytes 589840 | tf_op jit(solution)/shard_map/reduce_scatter | solution.py:327
  775.7 35.8 %reduce-scatter.18.cloned.1.call-done = bf16[192,1536]{1,0:T(8,128)(2,1)} async-done(((bf16[768,1536]{1,0:T(8,128)(2,1)}), bf16[192,1536]{1,0:T(8,128)(2,1)}) %reduce-scatter.18.cloned.1.call-update) | async-done | bytes 589840 | tf_op jit(solution)/shard_map/reduce_scatter | solution.py:330
  811.6 51.0 %reduce-scatter.20.cloned.1.call-done = bf16[384,1536]{1,0:T(8,128)(2,1)} async-done(((bf16[1536,1536]{1,0:T(8,128)(2,1)}), bf16[384,1536]{1,0:T(8,128)(2,1)}) %reduce-scatter.20.cloned.1.call-update) | async-done | bytes 1179664 | tf_op jit(solution)/shard_map/reduce_scatter | solution.py:333
  862.5 102.1 %reduce-scatter.22.cloned.1.call-done = bf16[1024,1536]{1,0:T(8,128)(2,1)} async-done(((bf16[4096,1536]{1,0:T(8,128)(2,1)}), bf16[1024,1536]{1,0:T(8,128)(2,1)}) %reduce-scatter.22.cloned.1.call-update) | async-done | bytes 3145744 | tf_op jit(solution)/shard_map/reduce_scatter | solution.py:274
  964.6 102.1 %reduce-scatter.24.cloned.1.call-done = bf16[1024,1536]{1,0:T(8,128)(2,1)} async-done(((bf16[4096,1536]{1,0:T(8,128)(2,1)}), bf16[1024,1536]{1,0:T(8,128)(2,1)}) %reduce-scatter.24.cloned.1.call-update) | async-done | bytes 3145744 | tf_op jit(solution)/shard_map/reduce_scatter | solution.py:277
  1066.7 102.1 %reduce-scatter.26.cloned.1.call-done = bf16[1024,1536]{1,0:T(8,128)(2,1)} async-done(((bf16[4096,1536]{1,0:T(8,128)(2,1)}), bf16[1024,1536]{1,0:T(8,128)(2,1)}) %reduce-scatter.26.cloned.1.call-update) | async-done | bytes 3145744 | tf_op jit(solution)/shard_map/reduce_scatter | solution.py:280
  1168.8 3.2 fusion.114
  1172.1 7.3 fusion.86
  1181.9 44.3 %all-reduce = (f32[1536]{0:T(1024)}, f32[1536]{0:T(1024)}) all-reduce(f32[1536]{0:T(1024)S(1)} %get-tuple-element.788, f32[1536]{0:T(1024)S(1)} %get-tuple-element.786), channel_id=1, replica_groups=mesh['fsdp'=4,'ctx'=8] {'fsdp','ctx'}, use_global_device_ids=true, to_apply=%region_18.19 | all-reduce | flops 3072 | bytes 24576 | tf_op jit(solution)/shard_map/psum | solution.py:355
  1227.4 81.9 %all-gather.32.cloned.1.call-done = bf16[3072,1536]{1,0:T(8,128)(2,1)} async-done(((bf16[384,1536]{1,0:T(8,128)(2,1)}), bf16[3072,1536]{1,0:T(8,128)(2,1)}) %all-gather.32.cloned.1.call-update) | async-done | bytes 9437200 | tf_op jit(solution)/shard_map/all_gather | solution.py:345
  1309.4 5.7 reduce_sum.97
  1316.8 358.2 %all-reduce.4.cloned.1.call-done = (bf16[192,1536]{1,0:T(8,128)(2,1)}, bf16[192,1536]{1,0:T(8,128)(2,1)}, bf16[384,1536]{1,0:T(8,128)(2,1)}, bf16[1024,1536]{1,0...) async-done(((bf16[192,1536]{1,0:T(8,128)(2,1)}, bf16[192,1536]{1,0:T(8,128)(2,1)}, bf16[384,1536]{1,0:T(8,128)(2,1)}, bf16[1024,1536]{1,0:T(8,128)(2,1)}, ...) | async-done | bytes 11796496 | tf_op jit(solution)/shard_map/psum | solution.py:348
  1675.0 5.6 convert_element_type.221
  1680.6 3.6 convert_element_type.223
  1684.2 3.6 convert_element_type.225
  (201 shorter events, 49.7 us)
Async XLA Ops:
  7.2 54.8 %copy-start.2 = (bf16[128,1536]{1,0:T(8,128)(2,1)S(1)}, bf16[128,1536]{1,0:T(8,128)(2,1)}, u32[]{:S(2)}) copy-start(bf16[128,1536]{1,0:T(8,128)(2,1)} %param.20) | copy-start | bytes 1179652
  7.2 33.2 %copy-start.32 = (s32[128]{0:T(128)S(1)}, s32[128]{0:T(128)}, u32[]{:S(2)}) copy-start(s32[128]{0:T(128)} %param.21) | copy-start | bytes 1540
  7.2 29.2 %all-gather.14.cloned.1.call-start = ((), (), s32[]{:S(2)}) async-start(), calls=%async_computation.9 | async-start | bytes 2949120 | tf_op jit(solution)/shard_map/all_gather | solution.py:208
  7.9 54.1 %all-gather.16.cloned.1.call-start = ((), (), s32[]{:S(2)}) async-start(), calls=%async_computation.10 | async-start | bytes 2949120 | tf_op jit(solution)/shard_map/all_gather | solution.py:207
  8.7 100.3 %all-gather.30.cloned.1.call-start = ((), (), s32[]{:S(2)}) async-start(), calls=%async_computation.24 | async-start | bytes 1769472 | tf_op jit(solution)/shard_map/all_gather | solution.py:240
  39.8 106.5 %all-gather.20.cloned.1.call-start = ((), (), s32[]{:S(2)}) async-start(), calls=%async_computation.12 | async-start | bytes 5898240 | tf_op jit(solution)/shard_map/all_gather | solution.py:206
  40.4 152.8 %all-gather.18.cloned.1.call-start = ((), (), s32[]{:S(2)}) async-start(), calls=%async_computation.11 | async-start | bytes 1769472 | tf_op jit(solution)/shard_map/all_gather | solution.py:239
  65.3 164.9 %all-gather.22.cloned.1.call-start = ((), (), s32[]{:S(2)}) async-start(), calls=%async_computation.13 | async-start | bytes 5898240 | tf_op jit(solution)/shard_map/all_gather | solution.py:209
  65.9 2.3 copy-start.33
  65.9 248.0 %all-gather.24.cloned.1.call-start = ((), (), s32[]{:S(2)}) async-start(), calls=%async_computation.14 | async-start | bytes 15728640 | tf_op jit(solution)/shard_map/all_gather | solution.py:214
  66.6 330.9 %all-gather.26.cloned.1.call-start = ((), (), s32[]{:S(2)}) async-start(), calls=%async_computation.15 | async-start | bytes 15728640 | tf_op jit(solution)/shard_map/all_gather | solution.py:215
  67.4 413.8 %all-gather.28.cloned.1.call-start = ((), (), s32[]{:S(2)}) async-start(), calls=%async_computation.16 | async-start | bytes 15728640 | tf_op jit(solution)/shard_map/all_gather | solution.py:216
  68.1 553.4 %reduce-scatter.28.cloned.1.call-start = ((), (), s32[]{:S(2)}) async-start(), calls=%async_computation.26 | async-start | bytes 1769472
  216.2 1.1 copy-start.22
  218.6 105.3 %copy-start.16 = (bf16[1,128,8,2,96]{1,4,3,2,0:T(8,128)(2,1)}, bf16[1,128,8,2,96]{1,4,3,2,0:T(8,128)(2,1)S(1)}, u32[]{:S(2)}) copy-start(bf16[1,128,8,2,96]{1,4,3,2,0:T(8,128)(2,1)S(1)} %convert_element_type.194) | copy-start | bytes 1179652
  233.4 272.9 %copy-start.4 = (f32[128,1536]{1,0:T(8,128)}, f32[128,1536]{1,0:T(8,128)S(1)}, u32[]{:S(2)}) copy-start(f32[128,1536]{1,0:T(8,128)S(1)} %get-tuple-element.886) | copy-start | bytes 2359300
  492.4 7.2 copy-start.12
  492.4 7.2 copy-start.10
  492.4 14.2 slice-start
  499.6 6.7 copy-start.25
  499.6 7.0 slice-start.1
  506.6 2.1 copy-start.6
  508.7 2.2 copy-start.23
  512.4 2.2 copy-start.23
  518.7 2.3 copy-start.30
  518.7 2.3 copy-start.24
  520.8 3.0 copy-start
  525.4 2.7 copy-start.1
  528.1 3.1 copy-start.31
  531.2 2.2 copy-start.30
  531.2 2.3 copy-start.24
  533.3 3.0 copy-start
  537.9 2.9 copy-start.1
  540.9 3.0 copy-start.31
  552.2 3.5 copy-start.15
  555.7 134.4 %reduce-scatter.30.cloned.1.call-start = ((), (), s32[]{:S(2)}) async-start(), calls=%async_computation.27 | async-start | bytes 1769472
  561.2 3.5 copy-start.3
  564.7 175.1 %reduce-scatter.14.cloned.1.call-start = ((), (), s32[]{:S(2)}) async-start(), calls=%async_computation.17 | async-start | bytes 5898240 | tf_op jit(solution)/shard_map/reduce_scatter | solution.py:324
  568.6 207.1 %reduce-scatter.16.cloned.1.call-start = ((), (), s32[]{:S(2)}) async-start(), calls=%async_computation.18 | async-start | bytes 2949120 | tf_op jit(solution)/shard_map/reduce_scatter | solution.py:327
  625.4 68.7 %copy-start.7 = (f32[128,1536]{1,0:T(8,128)S(1)}, f32[128,1536]{1,0:T(8,128)}, u32[]{:S(2)}) copy-start(f32[128,1536]{1,0:T(8,128)} %copy-done.6) | copy-start | bytes 2359300
  625.4 68.7 %copy-start.17 = (bf16[1,128,8,2,96]{1,4,3,2,0:T(8,128)(2,1)S(1)}, bf16[1,128,8,2,96]{1,4,3,2,0:T(8,128)(2,1)}, u32[]{:S(2)}) copy-start(bf16[1,128,8,2,96]{1,4,3,2,0:T(8,128)(2,1)} %copy-done.16) | copy-start | bytes 1179652
  625.5 186.1 %reduce-scatter.18.cloned.1.call-start = ((), (), s32[]{:S(2)}) async-start(), calls=%async_computation.19 | async-start | bytes 2949120 | tf_op jit(solution)/shard_map/reduce_scatter | solution.py:330
  691.6 6.3 copy-start.20
  693.9 168.6 %reduce-scatter.20.cloned.1.call-start = ((), (), s32[]{:S(2)}) async-start(), calls=%async_computation.20 | async-start | bytes 5898240 | tf_op jit(solution)/shard_map/reduce_scatter | solution.py:333
  697.9 1.2 copy-start.13
  697.9 266.7 %reduce-scatter.22.cloned.1.call-start = ((), (), s32[]{:S(2)}) async-start(), calls=%async_computation.21 | async-start | bytes 15728640 | tf_op jit(solution)/shard_map/reduce_scatter | solution.py:274
  705.6 1.2 copy-start.11
  705.7 361.0 %reduce-scatter.24.cloned.1.call-start = ((), (), s32[]{:S(2)}) async-start(), calls=%async_computation.22 | async-start | bytes 15728640 | tf_op jit(solution)/shard_map/reduce_scatter | solution.py:277
  713.5 1.2 copy-start.14
  713.5 1.3 copy-start.26
  713.5 455.3 %reduce-scatter.26.cloned.1.call-start = ((), (), s32[]{:S(2)}) async-start(), calls=%async_computation.23 | async-start | bytes 15728640 | tf_op jit(solution)/shard_map/reduce_scatter | solution.py:280
  721.3 588.1 %all-gather.32.cloned.1.call-start = ((), (), s32[]{:S(2)}) async-start(), calls=%async_computation.25 | async-start | bytes 10616832 | tf_op jit(solution)/shard_map/all_gather | solution.py:345
  739.8 935.2 %all-reduce.4.cloned.1.call-start = ((), (), s32[]{:S(2)}) async-start(), calls=%async_computation.28 | async-start | bytes 23592960 | tf_op jit(solution)/shard_map/psum | solution.py:348
  1168.8 3.2 copy-start.5
  1172.1 7.3 copy-start.9
  1179.4 1.8 copy-start.8
  1179.4 1.8 copy-start.21
  1675.0 5.6 copy-start.19
  1680.6 3.6 copy-start.18
  1684.2 3.6 copy-start.27
  1684.2 5.3 copy-start.29
  1687.8 2.9 copy-start.28
Sparse Core Ops, SparseCore 0:
  9.6 26.7 all-gather.13
  37.9 24.0 all-gather.15
  64.8 44.1 all-gather.29
  110.4 35.7 all-gather.19
  148.7 44.4 all-gather.17
  194.6 35.5 all-gather.21
  231.8 82.0 all-gather.23
  315.4 82.0 all-gather.25
  399.1 82.0 all-gather.27
  555.8 65.6 reduce-scatter.27
  625.5 64.5 reduce-scatter.29
  693.0 46.7 reduce-scatter.13
  742.9 32.8 reduce-scatter.15
  778.7 32.8 reduce-scatter.17
  814.5 47.9 reduce-scatter.19
  865.0 99.6 reduce-scatter.21
  967.1 99.6 reduce-scatter.23
  1069.2 99.6 reduce-scatter.25
  1171.0 138.3 all-gather.31
  1314.4 360.4 all-reduce.3
